TPU v7x, 32 devices: a whole 2x2x4 slice. The times are simulated.
32 devices in a mesh: seq: 8 (over z, y), batch: 4 (over x, core).
Axes of the slice: x: 2, y: 2, z: 4, core: 2. Of those that a mesh axis runs over, the one named last changes fastest.
Arguments:
- queries: bfloat16 [4, 4096, 16, 128], P('batch', 'seq'), may hold values from -5 to 5
- keys: bfloat16 [4, 4096, 16, 128], P('batch', 'seq'), may hold values from -5 to 5
- values: bfloat16 [4, 4096, 16, 128], P('batch', 'seq'), may hold values from -5 to 5
- keep_count: int32 [4, 16, 32], P('batch'), may hold values from 0 to 128
- query_map: bfloat16 [16, 128, 8], replicated, may hold values from -0.5 to 0.5
- key_map: bfloat16 [16, 128, 8], replicated, may hold values from -0.5 to 0.5
- cotangent: bfloat16 [4, 4096, 16, 128], P('batch', 'seq'), may hold values from -5 to 5
Outputs:
- attended: bfloat16 [4, 4096, 16, 128], P('batch', 'seq')
- grad_query_map: float32 [16, 128, 8], replicated
- grad_key_map: float32 [16, 128, 8], replicated
All inputs are finite; a program needn't handle non-finite values.
Results may differ from a plain program's by a relative error of at most 0.0035.
Values may be sent and summed in bfloat16 or wider, within the bound.
A program may use at most 128 MiB of HBM per device.

v0:
```python
import math
import jax
import jax.numpy as jnp
from jax import lax
from jax.sharding import PartitionSpec as P

TILE = 128
WINDOW = 256
HIGHEST = lax.Precision.HIGHEST
feature_shift = 1.5


def passed_along(value, axis, steps):
    count = lax.axis_size(axis)
    first, last = (max(0, -steps), min(count, count - steps))
    return lax.ppermute(value, axis, [(source, source + steps) for source in range(first, last)])


def prefix(shard, axis, combine, identity, reverse):
    peers, position = (lax.axis_size(axis), lax.axis_index(axis))
    everything = jax.tree.map(lambda part: lax.all_gather(part, axis), shard)
    start = jax.tree.map(
        lambda part, zero: jnp.broadcast_to(jnp.asarray(zero, part.dtype), part.shape),
        shard,
        identity,
    )

    def step(k, before):
        at = peers - 1 - k if reverse else k
        reached = at > position if reverse else at < position
        new = combine(before, jax.tree.map(lambda part: part[at], everything))
        return jax.tree.map(lambda a, b: jnp.where(reached, a, b), new, before)

    return lax.fori_loop(0, peers, step, start)


def add_pair(earlier, later):
    return (earlier[0] + later[0], earlier[1] + later[1])


def windowed(tiled, first, count, span):
    pieces = [
        lax.slice_in_dim(tiled, first + offset, first + offset + count, axis=0)
        for offset in range(span)
    ]
    return jnp.concatenate(pieces, 1)


def body(queries, keys, values, keep_count, query_map, key_map, cotangent):
    q_rows = queries[0]
    k_rows = keys[0]
    v_rows = values[0]
    cot_rows = cotangent[0].astype(jnp.float32)
    tokens, heads, width = q_rows.shape
    rank = query_map.shape[2]
    tiles_dev = tokens // TILE
    span = WINDOW // TILE
    scale = 1.0 / math.sqrt(width)
    index = lax.axis_index("seq")
    halo_rows = WINDOW - TILE
    prev_keys, prev_values = passed_along(
        (k_rows[tokens - halo_rows :], v_rows[tokens - halo_rows :]), "seq", 1
    )
    halo_tiles = halo_rows // TILE
    ext_tiles = halo_tiles + tiles_dev
    ext_rows = halo_rows + tokens
    ext_keys = jnp.concatenate([prev_keys, k_rows], 0)
    ext_values = jnp.concatenate([prev_values, v_rows], 0)
    counts = keep_count[0]
    padded_counts = jnp.concatenate([jnp.zeros((heads, tiles_dev), jnp.int32), counts], 1)
    count_start = index * tiles_dev + tiles_dev - halo_tiles
    ext_counts = lax.dynamic_slice_in_dim(padded_counts, count_start, ext_tiles, 1)
    local = jnp.arange(ext_rows, dtype=jnp.int32)
    key_pos = index * tokens - halo_rows + local
    valid = key_pos >= 0
    within = local % TILE
    kept = within[None, :] < jnp.repeat(ext_counts, TILE, axis=1)
    evicted = valid[None, :] & jnp.logical_not(kept)
    pre_q = (
        jnp.einsum("thd,hdr->thr", q_rows, query_map, preferred_element_type=jnp.float32)
        - feature_shift
    )
    pre_k = (
        jnp.einsum("thd,hdr->thr", ext_keys, key_map, preferred_element_type=jnp.float32)
        - feature_shift
    )
    feat_q = jax.nn.softplus(pre_q)
    feat_k = jax.nn.softplus(pre_k)
    valid_f = valid.astype(jnp.float32)[:, None, None]
    evict_f = evicted.T.astype(jnp.float32)[:, :, None]
    v_tiles = ext_values.astype(jnp.float32).reshape(ext_tiles, TILE, heads, width)

    def tile_state(feat):
        tiled = feat.reshape(ext_tiles, TILE, heads, rank)
        return (jnp.einsum("nthr,nthd->nhrd", tiled, v_tiles, precision=HIGHEST), jnp.sum(tiled, 1))

    all_state, all_norm = tile_state(feat_k * valid_f)
    ev_state, ev_norm = tile_state(feat_k * evict_f)
    q_tile = jnp.arange(tiles_dev, dtype=jnp.int32)[:, None] + halo_tiles
    k_tile = jnp.arange(ext_tiles, dtype=jnp.int32)[None, :]
    in_halo = (k_tile < halo_tiles).astype(jnp.float32)
    far_mix = (k_tile < q_tile - span + 1).astype(jnp.float32)
    near_mix = ((k_tile >= q_tile - span + 1) & (k_tile < q_tile)).astype(jnp.float32)
    far_coef = far_mix * (1.0 - in_halo) - near_mix * in_halo
    carried_state = jnp.sum(all_state[halo_tiles:], 0)
    carried_norm = jnp.sum(all_norm[halo_tiles:], 0)
    far_state, far_norm = prefix(
        (carried_state, carried_norm),
        "seq",
        add_pair,
        (jnp.zeros_like(carried_state), jnp.zeros_like(carried_norm)),
        False,
    )
    state = (
        far_state[None]
        + jnp.einsum("jn,nhrd->jhrd", far_coef, all_state, precision=HIGHEST)
        + jnp.einsum("jn,nhrd->jhrd", near_mix, ev_state, precision=HIGHEST)
    )
    norm = (
        far_norm[None]
        + jnp.einsum("jn,nhr->jhr", far_coef, all_norm, precision=HIGHEST)
        + jnp.einsum("jn,nhr->jhr", near_mix, ev_norm, precision=HIGHEST)
    )
    first_tile = halo_tiles - span + 1
    key_window = windowed(
        ext_keys.reshape(ext_tiles, TILE, heads, width), first_tile, tiles_dev, span
    )
    value_window = windowed(
        ext_values.reshape(ext_tiles, TILE, heads, width), first_tile, tiles_dev, span
    )
    allowed = (kept & valid[None, :]).T.reshape(ext_tiles, TILE, heads)
    allowed_window = windowed(allowed, first_tile, tiles_dev, span).transpose(0, 2, 1)
    slot = jnp.arange(span * TILE, dtype=jnp.int32)
    own_slot = slot >= (span - 1) * TILE
    causal = slot[None, :] - (span - 1) * TILE <= jnp.arange(TILE, dtype=jnp.int32)[:, None]
    live_pairs = jnp.where(
        own_slot[None, None, None, :], causal[None, None], allowed_window[:, :, None, :]
    )
    q_tiles = q_rows.reshape(tiles_dev, TILE, heads, width)
    scores = (
        jnp.einsum("nqhd,nkhd->nhqk", q_tiles, key_window, preferred_element_type=jnp.float32)
        * scale
    )
    row_max = jnp.max(jnp.where(live_pairs, scores, -jnp.inf), -1)
    weights = jnp.where(live_pairs, jnp.exp(scores - row_max[..., None]), 0.0)
    denom = jnp.sum(weights, -1).transpose(0, 2, 1).reshape(tokens, heads)
    numer = jnp.einsum(
        "nhqk,nkhd->nqhd",
        weights.astype(jnp.bfloat16),
        value_window,
        preferred_element_type=jnp.float32,
    ).reshape(tokens, heads, width)
    decay = jnp.exp(-row_max.transpose(0, 2, 1).reshape(tokens, heads))
    feat_qt = feat_q.reshape(tiles_dev, TILE, heads, rank)
    kernel_num = jnp.einsum("nthr,nhrd->nthd", feat_qt, state, precision=HIGHEST).reshape(
        tokens, heads, width
    )
    kernel_den = jnp.einsum("nthr,nhr->nth", feat_qt, norm, precision=HIGHEST).reshape(
        tokens, heads
    )
    total = denom + decay * kernel_den
    out = (numer + decay[..., None] * kernel_num) / total[..., None]
    delta = cot_rows / total[..., None]
    ratio_grad = -jnp.sum(delta * out, -1)
    grad_num = (decay[..., None] * delta).reshape(tiles_dev, TILE, heads, width)
    grad_den = (decay * ratio_grad).reshape(tiles_dev, TILE, heads)
    grad_fq = (
        jnp.einsum("nthd,nhrd->nthr", grad_num, state, precision=HIGHEST)
        + grad_den[..., None] * norm[:, None]
    )
    d_state = jnp.einsum("nthr,nthd->nhrd", feat_qt, grad_num, precision=HIGHEST)
    d_norm = jnp.einsum("nthr,nth->nhr", feat_qt, grad_den, precision=HIGHEST)
    own_state = jnp.sum(d_state, 0)
    own_norm = jnp.sum(d_norm, 0)
    after_state, after_norm = prefix(
        (own_state, own_norm),
        "seq",
        add_pair,
        (jnp.zeros_like(own_state), jnp.zeros_like(own_norm)),
        True,
    )
    own_tiles = (jnp.arange(ext_tiles, dtype=jnp.int32) >= halo_tiles).astype(jnp.float32)
    d_all = (
        jnp.einsum("jn,jhrd->nhrd", far_coef, d_state, precision=HIGHEST)
        + own_tiles[:, None, None, None] * after_state[None]
    )
    d_alln = (
        jnp.einsum("jn,jhr->nhr", far_coef, d_norm, precision=HIGHEST)
        + own_tiles[:, None, None] * after_norm[None]
    )
    d_ev = jnp.einsum("jn,jhrd->nhrd", near_mix, d_state, precision=HIGHEST)
    d_evn = jnp.einsum("jn,jhr->nhr", near_mix, d_norm, precision=HIGHEST)
    grad_all = jnp.einsum("nhrd,nthd->nthr", d_all, v_tiles, precision=HIGHEST) + d_alln[:, None]
    grad_ev = jnp.einsum("nhrd,nthd->nthr", d_ev, v_tiles, precision=HIGHEST) + d_evn[:, None]
    grad_fk = valid_f * grad_all.reshape(ext_rows, heads, rank) + evict_f * grad_ev.reshape(
        ext_rows, heads, rank
    )
    grad_pre_k = grad_fk * jax.nn.sigmoid(pre_k)
    grad_pre_q = grad_fq.reshape(tokens, heads, rank) * jax.nn.sigmoid(pre_q)
    grad_q = jnp.einsum("thd,thr->hdr", q_rows.astype(jnp.float32), grad_pre_q, precision=HIGHEST)
    grad_k = jnp.einsum("thd,thr->hdr", ext_keys.astype(jnp.float32), grad_pre_k, precision=HIGHEST)
    grad_q, grad_k = lax.psum((grad_q, grad_k), ("seq", "batch"))
    return (out.astype(jnp.bfloat16)[None], grad_q, grad_k)


def solution(mesh):
    placed = (
        P("batch", "seq", None, None),
        P("batch", "seq", None, None),
        P("batch", "seq", None, None),
        P("batch", None, None),
        P(),
        P(),
        P("batch", "seq", None, None),
    )
    return jax.shard_map(
        body,
        mesh=mesh,
        in_specs=placed,
        out_specs=(P("batch", "seq", None, None), P(), P()),
        check_vma=False,
    )
```

profile of v0, /device:TPU:0, one launch (start us, length us, event | category | flops | bytes accessed | tf_op | source)
XLA Modules:
  0.0 420.2 jit_solution(9056168187303462686)
XLA Ops:
  7.2 2.3 copy.332
  9.5 1.4 copy-done.4
  11.7 5.7 %collective-permute-start.1 = (bf16[128,16,128]{2,0,1:T(8,128)(2,1)}, bf16[128,16,128]{2,0,1:T(8,128)(2,1)}, u32[]{:S(2)}, u32[]{:S(2)}) collective-permute-start(bf16[128,16,128]{2,0,1:T(8,128)(2,1)} %slice_bitcast_fusion), channel_id=1, source_target_pairs={{0,4},{4,8},{8,12},{12,16},{16,20},{20,24},{24,28},{1,5},{5,9},{9,... | collective-permute-start | bytes 1572872 | tf_op jit(solution)/shard_map/ppermute | solution.py:16
  17.4 1.9 slice_bitcast_fusion.1
  19.3 2.7 collective-permute-start
  26.0 3.5 copy.177
  29.5 1.9 copy.171
  31.4 2.4 convert.3
  33.8 1.5 fusion.73
  35.3 2.0 fusion.65
  38.1 0.9 fusion.171
  39.7 1.9 pad_maximum_fusion
  41.6 1.5 copy-done.1
  43.1 2.1 fusion.44
  45.3 35.2 %all-gather = f32[128,8,128]{2,1,0:T(8,128)} all-gather(f32[16,8,128]{2,1,0:T(8,128)S(1)} %slice_reduce_fusion), channel_id=2, replica_groups=mesh['seq'=8,'batch'=4] {'seq'}, dimensions={0}, use_global_device_ids=true | all-gather | bytes 589824 | tf_op jit(solution)/shard_map/all_gather | solution.py:21
  80.6 30.6 %all-gather.4 = f32[8,16,8]{1,2,0:T(8,128)S(1)} all-gather(f32[1,16,8]{1,2,0:T(8,128)S(1)} %bitcast.246), channel_id=3, replica_groups=mesh['seq'=8,'batch'=4] {'seq'}, dimensions={0}, use_global_device_ids=true | all-gather | bytes 4608 | tf_op jit(solution)/shard_map/all_gather | solution.py:21
  111.2 7.7 %while.34 = (s32[]{:T(128)}, f32[16,8,128]{2,1,0:T(8,128)S(1)}, f32[16,8]{0,1:T(8,128)S(1)}, s32[]{:T(128)}, f32[8,16,8,128]{3,2,1,0:T(8,128)}, /*index=5*/f32[8,16,8]{1,2,0:T(8,128)S(1)}, s32[]{:T(128)}, s32[]{:T(128)}) while((s32[]{:T(128)}, f32[16,8,128]{2,1,0:T(8,128)S(1)}, f32[16,8]{0,1:T(8,128)S(1)}, s32[]{:T(128)}, ...), condition=%wide.region_5.6_spmd.clone, body=%wide.region_4.5_spmd.clone.sunk | while | flops 49540 | bytes 198259 | solution.py:34
  112.1 0.9 add_select_fusion.9
  113.0 0.9 add_select_fusion.9
  113.9 0.9 add_select_fusion.9
  114.8 0.9 add_select_fusion.9
  118.9 3.9 fusion.42
  124.9 6.7 %convolution_bitcast_fusion = f32[4,128,16,128]{3,1,2,0:T(8,128)S(1)} fusion(f32[4,16,8,128]{3,0,2,1:T(4,128)S(1)} %fusion.66, f32[512,16,8]{0,2,1:T(8,128)S(1)} %copy-done.13), kind=kOutput, calls=%fused_computation.42 | convolution fusion | flops 101056512 | bytes 4718592 | tf_op jit(solution)/shard_map/nthr,nhrd->nthd/dot_general | solution.py:155
  131.6 4.5 %copy.193 = f32[4,128,16,128]{3,2,1,0:T(8,128)} copy(f32[4,128,16,128]{3,1,2,0:T(8,128)S(1)} %convolution_bitcast_fusion) | data formatting | bytes 8388608 | tf_op jit(solution)/shard_map/nthr,nhrd->nthd/transpose | solution.py:155
  138.2 1.7 pad_maximum_fusion.2
  139.9 2.9 fusion
  143.5 4.1 fusion.2
  148.4 1.7 fusion.32
  150.7 1.6 copy-done.10
  152.3 6.3 %fusion.27 = f32[4,128,16,128]{3,1,2,0:T(8,128)S(1)} fusion(f32[4,16,256,128]{3,2,1,0:T(8,128)S(1)} %copy-done.10, f32[4,16,128]{2,1,0:T(8,128)S(1)} %get-tuple-element.356, pred[4,16,256]{2,1,0:T(8,128)(4,1)S(1)} %copy-done.26, pred[128,256]{0,1:T(8,128)(4,1)S(1)} %copy-done.21, pred[256]{0:T(512)(128)(4,1)S(1)} %copy-done.42, ...), kind=kOutput, calls=%fused_computation.41 | convolution fusion | flops 555745280 | bytes 16859392 | tf_op jit(solution)/shard_map/nhqk,nkhd->nqhd/dot_general | solution.py:147
  158.6 4.4 %copy.180 = f32[4,128,16,128]{3,2,1,0:T(8,128)} copy(f32[4,128,16,128]{3,1,2,0:T(8,128)S(1)} %fusion.27) | data formatting | bytes 8388608 | tf_op jit(solution)/shard_map/nhqk,nkhd->nqhd/transpose | solution.py:147
  163.1 6.9 %fusion.14 = f32[512,16,128]{2,1,0:T(8,128)S(1)} fusion(f32[4,128,16,128]{3,2,1,0:T(8,128)} %copy.193, f32[4,128,16,128]{3,2,1,0:T(8,128)} %copy.180, f32[512,16]{1,0:T(8,128)S(1)} %copy.182, f32[512,16]{1,0:T(8,128)S(1)} %copy.198), kind=kLoop, calls=%fused_computation.21 | loop fusion | flops 3145728 | bytes 12648448 | tf_op jit(solution)/shard_map/div | solution.py:162
  170.0 14.1 %fusion.23 = f32[512,16]{1,0:T(8,128)S(1)} fusion(f32[512,16,128]{2,1,0:T(8,128)S(1)} %fusion.14, f32[512,16]{1,0:T(8,128)S(1)} %copy.198, bf16[1,512,16,128]{3,2,1,0:T(8,128)(2,1)S(1)} %copy-done.8), kind=kLoop, calls=%fused_computation.33 | loop fusion | flops 4186112 | bytes 6356992 | tf_op jit(solution)/shard_map/reduce_sum | solution.py:164
  185.1 0.9 fusion.122
  186.7 7.5 %fusion.174 = (f32[16,8,128]{2,1,0:T(8,128)S(1)}, f32[4,16,8,128]{3,2,1,0:T(8,128)}) fusion(f32[4,128,16,128]{3,2,1,0:T(8,128)} %convert.3, f32[4,128,16]{1,2,0:T(8,128)S(1)} %get-tuple-element.351, f32[4,128,16]{1,2,0:T(8,128)S(1)} %copy-done.28, f32[512,16,8]{0,2,1:T(8,128)S(1)} %copy-done.14), kind=kOutput, calls=%fused_computation.200 | convolution fusion | flops 103202816 | bytes 4849664 | tf_op jit(solution)/shard_map/nthr,nthd->nhrd/dot_general | solution.py:171
  194.2 31.2 %all-gather.2 = f32[128,8,128]{2,1,0:T(8,128)S(1)} all-gather(f32[16,8,128]{2,1,0:T(8,128)S(1)} %get-tuple-element.358), channel_id=4, replica_groups=mesh['seq'=8,'batch'=4] {'seq'}, dimensions={0}, use_global_device_ids=true | all-gather | bytes 589824 | tf_op jit(solution)/shard_map/all_gather | solution.py:21
  225.4 30.6 %all-gather.5 = f32[8,16,8]{1,2,0:T(8,128)S(1)} all-gather(f32[1,16,8]{1,2,0:T(8,128)S(1)} %bitcast.245), channel_id=5, replica_groups=mesh['seq'=8,'batch'=4] {'seq'}, dimensions={0}, use_global_device_ids=true | all-gather | bytes 4608 | tf_op jit(solution)/shard_map/all_gather | solution.py:21
  257.1 1.6 fusion.106
  258.7 2.6 convolution_add_fusion
  262.2 9.5 %fusion.76 = f32[4,128,16,8]{1,3,2,0:T(8,128)S(1)} fusion(f32[4,128,16,128]{3,2,1,0:T(8,128)} %convert.3, f32[4,128,16]{1,2,0:T(8,128)} %copy-done.31, f32[4,128,16]{1,2,0:T(8,128)} %get-tuple-element.352, f32[4,16,8,128]{3,0,2,1:T(4,128)} %copy-done.15, f32[4,16,8]{2,1,0:T(8,128)} %copy.207, f32[4,128,16]{1,2,0:T(8,128)} %copy-done.30), kind=kOutput, calls=%fused_computation.74 | convolution fusion | flops 102891520 | bytes 4818944 | tf_op jit(solution)/shard_map/nthd,nhrd->nthr/dot_general | solution.py:168
  271.7 2.0 fusion.79
  273.7 4.1 fusion.51
  277.9 4.1 fusion.57
  282.1 3.1 fusion.47
  285.1 7.2 %fusion.18 = bf16[1,512,16,128]{3,2,1,0:T(8,128)(2,1)} fusion(f32[512,16]{1,0:T(8,128)S(1)} %copy.198, f32[512,16]{1,0:T(8,128)S(1)} %copy.182, f32[1,512,16,128]{3,2,1,0:T(8,128)} %bitcast.221, f32[1,512,16,128]{3,2,1,0:T(8,128)} %bitcast.222), kind=kLoop, calls=%fused_computation.27 | loop fusion | flops 4194304 | bytes 10551296 | tf_op jit(solution)/shard_map/convert_element_type | solution.py:203
  292.4 117.7 %all-reduce.4.cloned.1.call-done = (f32[16,128,8]{1,2,0:T(8,128)}, f32[16,128,8]{1,2,0:T(8,128)}) async-done(((f32[16,128,8]{1,2,0:T(8,128)}, f32[16,128,8]{1,2,0:T(8,128)}), (f32[16,128,8]{1,2,0:T(8,128)}, f32[16,128,8]{1,2,0:T(8,128)})) %all-reduce.4.cloned.1.call-update) | async-done | bytes 131088 | tf_op jit(solution)/shard_map/psum | solution.py:202
  410.1 1.5 copy.353
  411.5 1.5 copy.354
  (170 shorter events, 19.9 us)
Async XLA Ops:
  7.2 26.6 %copy-start = (bf16[1,512,16,128]{3,2,1,0:T(8,128)(2,1)S(1)}, bf16[1,512,16,128]{3,2,1,0:T(8,128)(2,1)}, u32[]{:S(2)}) copy-start(bf16[1,512,16,128]{3,2,1,0:T(8,128)(2,1)} %param.11) | copy-start | bytes 6291460
  7.2 16.6 %copy-start.37 = (s32[1,16,32]{2,1,0:T(8,128)S(1)}, s32[1,16,32]{2,1,0:T(8,128)}, u32[]{:S(2)}) copy-start(s32[1,16,32]{2,1,0:T(8,128)} %param.14) | copy-start | bytes 6148
  7.2 402.9 %all-reduce.4.cloned.1.call-start = ((), (), s32[]{:S(2)}) async-start(), calls=%async_computation | async-start | bytes 262144 | tf_op jit(solution)/shard_map/psum | solution.py:202
  9.5 1.4 copy-start.4
  11.7 23.6 %collective-permute-start.1 = (bf16[128,16,128]{2,0,1:T(8,128)(2,1)}, bf16[128,16,128]{2,0,1:T(8,128)(2,1)}, u32[]{:S(2)}, u32[]{:S(2)}) collective-permute-start(bf16[128,16,128]{2,0,1:T(8,128)(2,1)} %slice_bitcast_fusion), channel_id=1, source_target_pairs={{0,4},{4,8},{8,12},{12,16},{16,20},{20,24},{24,28},{1,5},{5,9},{9,... | collective-permute-start | bytes 1572872 | tf_op jit(solution)/shard_map/ppermute | solution.py:16
  19.3 20.4 %collective-permute-start = (bf16[128,16,128]{2,1,0:T(8,128)(2,1)}, bf16[128,16,128]{2,1,0:T(8,128)(2,1)S(1)}, u32[]{:S(2)}, u32[]{:S(2)}) collective-permute-start(bf16[128,16,128]{2,1,0:T(8,128)(2,1)} %slice_bitcast_fusion.1), channel_id=1, source_target_pairs={{0,4},{4,8},{8,12},{12,16},{16,20},{20,24},{24,28},{1,5},{5,9},{9,... | collective-permute-start | bytes 1572872 | tf_op jit(solution)/shard_map/ppermute | solution.py:16
  22.0 15.3 %copy-start.32 = (f32[640]{0:T(1024)}, f32[640]{0:T(1024)S(1)}, u32[]{:S(2)}) copy-start(f32[640]{0:T(1024)S(1)} %fusion.149) | copy-start | bytes 7684
  22.0 114.2 %copy-start.34 = (s32[4]{0:T(128)}, s32[4]{0:T(128)S(1)}, u32[]{:S(2)}) copy-start(s32[4]{0:T(128)S(1)} %iota_add_fusion.1) | copy-start | bytes 52
  25.4 4.1 copy-start.3
  29.5 1.9 copy-start.7
  31.4 2.4 copy-start.27
  31.4 4.0 copy-start.5
  31.4 4.0 copy-start.44
  33.8 3.5 copy-start.19
  37.3 0.7 copy-start.17
  39.7 3.4 copy-start.12
  41.6 1.5 copy-start.1
  111.2 12.2 %copy-start.38 = (f32[5]{0:T(128)S(1)}, f32[5]{0:T(128)}, u32[]{:S(2)}) copy-start(f32[5]{0:T(128)} %broadcast_subtract_fusion) | copy-start | bytes 64
  111.2 12.2 %copy-start.40 = (f32[5]{0:T(128)S(1)}, f32[5]{0:T(128)}, u32[]{:S(2)}) copy-start(f32[5]{0:T(128)} %compare_convert_fusion.1) | copy-start | bytes 64
  118.9 6.0 %copy-start.13 = (f32[512,16,8]{0,2,1:T(8,128)S(1)}, f32[512,16,8]{0,2,1:T(8,128)}, u32[]{:S(2)}) copy-start(f32[512,16,8]{0,2,1:T(8,128)} %fusion.73) | copy-start | bytes 786436
  124.2 0.7 copy-start.15
  131.6 4.7 %copy-start.29 = (f32[5,16,8]{1,0,2:T(8,128)S(1)}, f32[5,16,8]{1,0,2:T(8,128)}, u32[]{:S(2)}) copy-start(f32[5,16,8]{1,0,2:T(8,128)} %copy.195) | copy-start | bytes 7684
  131.6 5.8 %copy-start.14 = (f32[512,16,8]{0,2,1:T(8,128)S(1)}, f32[512,16,8]{0,2,1:T(8,128)}, u32[]{:S(2)}) copy-start(f32[512,16,8]{0,2,1:T(8,128)} %fusion.73) | copy-start | bytes 786436
  137.5 2.4 copy-start.11
  137.5 2.4 copy-start.21
  137.5 2.4 copy-start.26
  137.5 2.4 copy-start.42
  138.2 10.1 %copy-start.23 = (f32[4,16,1,128]{3,2,1,0:T(1,128)}, f32[4,16,1,128]{3,2,1,0:T(1,128)S(1)}, u32[]{:S(2)}) copy-start(f32[4,16,1,128]{3,2,1,0:T(1,128)S(1)} %fusion.112) | copy-start | bytes 98308
  142.8 4.8 %copy-start.9 = (f32[4,16,256,128]{3,2,1,0:T(8,128)}, f32[4,16,256,128]{3,2,1,0:T(8,128)S(1)}, u32[]{:S(2)}) copy-start(f32[4,16,256,128]{3,2,1,0:T(8,128)S(1)} %get-tuple-element.357) | copy-start | bytes 25165828
  148.4 3.9 copy-start.10
  158.6 4.4 %copy-start.22 = (f32[4,2,8,128]{3,2,0,1:T(8,128)S(1)}, f32[4,2,8,128]{3,2,0,1:T(8,128)}, u32[]{:S(2)}) copy-start(f32[4,2,8,128]{3,2,0,1:T(8,128)} %copy.331) | copy-start | bytes 98308
  163.1 6.9 %copy-start.8 = (bf16[1,512,16,128]{3,2,1,0:T(8,128)(2,1)S(1)}, bf16[1,512,16,128]{3,2,1,0:T(8,128)(2,1)}, u32[]{:S(2)}) copy-start(bf16[1,512,16,128]{3,2,1,0:T(8,128)(2,1)} %param.17) | copy-start | bytes 6291460
  170.0 14.2 %copy-start.24 = (f32[4,16,1,128]{3,2,1,0:T(1,128)S(1)}, f32[4,16,1,128]{3,2,1,0:T(1,128)}, u32[]{:S(2)}) copy-start(f32[4,16,1,128]{3,2,1,0:T(1,128)} %copy-done.23) | copy-start | bytes 98308
  170.0 15.0 %copy-start.35 = (s32[4]{0:T(128)S(1)}, s32[4]{0:T(128)}, u32[]{:S(2)}) copy-start(s32[4]{0:T(128)} %copy-done.34) | copy-start | bytes 52
  170.0 16.6 %copy-start.28 = (f32[4,128,16]{1,2,0:T(8,128)S(1)}, f32[4,128,16]{1,2,0:T(8,128)}, u32[]{:S(2)}) copy-start(f32[4,128,16]{1,2,0:T(8,128)} %get-tuple-element.352) | copy-start | bytes 98308
  184.3 9.9 %copy-start.30 = (f32[4,128,16]{1,2,0:T(8,128)}, f32[4,128,16]{1,2,0:T(8,128)S(1)}, u32[]{:S(2)}) copy-start(f32[4,128,16]{1,2,0:T(8,128)S(1)} %get-tuple-element.350) | copy-start | bytes 98308
  184.3 9.9 %copy-start.31 = (f32[4,128,16]{1,2,0:T(8,128)}, f32[4,128,16]{1,2,0:T(8,128)S(1)}, u32[]{:S(2)}) copy-start(f32[4,128,16]{1,2,0:T(8,128)S(1)} %get-tuple-element.351) | copy-start | bytes 98308
  186.6 69.3 %copy-start.25 = (f32[16,8]{0,1:T(8,128)S(1)}, f32[16,8]{0,1:T(8,128)}, u32[]{:S(2)}) copy-start(f32[16,8]{0,1:T(8,128)} %custom-call.3) | copy-start | bytes 1540
  186.6 70.1 %copy-start.36 = (s32[4]{0:T(128)S(1)}, s32[4]{0:T(128)}, u32[]{:S(2)}) copy-start(s32[4]{0:T(128)} %copy-done.34) | copy-start | bytes 52
  186.6 70.1 %copy-start.39 = (f32[5]{0:T(128)S(1)}, f32[5]{0:T(128)}, u32[]{:S(2)}) copy-start(f32[5]{0:T(128)} %broadcast_subtract_fusion) | copy-start | bytes 64
  186.6 70.1 %copy-start.41 = (f32[5]{0:T(128)S(1)}, f32[5]{0:T(128)}, u32[]{:S(2)}) copy-start(f32[5]{0:T(128)} %compare_convert_fusion.1) | copy-start | bytes 64
  186.6 70.1 %copy-start.43 = (f32[5]{0:T(128)S(1)}, f32[5]{0:T(128)}, u32[]{:S(2)}) copy-start(f32[5]{0:T(128)} %compare_convert_fusion) | copy-start | bytes 64
  271.7 2.0 copy-start.2
  271.7 2.0 copy-start.16
  277.8 4.2 copy-start.6
  277.8 4.2 copy-start.18
  277.8 4.2 copy-start.20
  277.9 4.2 %copy-start.33 = (f32[640]{0:T(1024)S(1)}, f32[640]{0:T(1024)}, u32[]{:S(2)}) copy-start(f32[640]{0:T(1024)} %copy-done.32) | copy-start | bytes 7684
Sparse Core Ops, SparseCore 0:
  285.3 124.7 all-reduce.3
where the time goes:
time: 427 us; the launch traced here: 420 us
  blocking collectives  128 us (30%)
  waiting for transfers between devices  118 us (28%)
  matrix products  64.9 us (15%)
  other arithmetic  52 us (12%)
  local copies, waits for them, and re-layouts  33.3 us (8%)
  between operations  15.1 us (4%)
  starting transfers between devices  8.39 us (2%)
    all_gather x4, blocking collectives, prefix(): everything = jax.tree.map(lambda part: lax.all_gather(part, axis), shard)  128 us
    psum x1, waiting for transfers between devices, body(): grad_q, grad_k = lax.psum((grad_q, grad_k), ('seq', 'batch'))  118 us
    reduce_sum x1, other arithmetic, body(): ratio_grad = -jnp.sum(delta * out, -1)  14.1 us
    unnamed x93, local copies, waits for them, and re-layouts  11.3 us
    dot_general x1, matrix products, body(): jnp.einsum('nthd,nhrd->nthr', grad_num, state, precision=HIGHEST)  9.54 us
  transfers between devices with their start and end apart: 3, of which 1 were waited for; matrix products, arithmetic and copies ran while one was open for 6% of the time, Pallas kernels for 0%

commit v1 on v0

--- a/solution.py
+++ b/solution.py
@@ -199,7 +199,7 @@
     grad_pre_q = grad_fq.reshape(tokens, heads, rank) * jax.nn.sigmoid(pre_q)
     grad_q = jnp.einsum("thd,thr->hdr", q_rows.astype(jnp.float32), grad_pre_q, precision=HIGHEST)
     grad_k = jnp.einsum("thd,thr->hdr", ext_keys.astype(jnp.float32), grad_pre_k, precision=HIGHEST)
-    grad_q, grad_k = lax.psum((grad_q, grad_k), ("seq", "batch"))
+    grad_q, grad_k = lax.psum(lax.psum((grad_q, grad_k), "batch"), "seq")
     return (out.astype(jnp.bfloat16)[None], grad_q, grad_k)
 
 

time: 427 us -> 408 us (0.956)
  waiting for transfers between devices: 118 us -> 98.8 us
    psum x1 -> x2, waiting for transfers between devices: 118 us -> 98.7 us  [body(): grad_q, grad_k = lax.psum(lax.psum((grad_q, grad_k), 'batch'), 'seq')]
  transfers between devices with their start and end apart: 3 -> 4, of which waited for: 1 -> 2; matrix products, arithmetic and copies ran while one was open for 6% -> 6% of each run, Pallas kernels for 0% -> 0%
where the time goes in v1:
time: 408 us; the launch traced here: 401 us
  blocking collectives  128 us (31%)
  waiting for transfers between devices  98.8 us (24%)
  matrix products  64.9 us (16%)
  other arithmetic  51.9 us (13%)
  local copies, waits for them, and re-layouts  33.3 us (8%)
  between operations  15.1 us (4%)
  starting transfers between devices  8.43 us (2%)
    all_gather x4, blocking collectives, prefix(): everything = jax.tree.map(lambda part: lax.all_gather(part, axis), shard)  128 us
    psum x2, waiting for transfers between devices, body(): grad_q, grad_k = lax.psum(lax.psum((grad_q, grad_k), 'batch'), 'seq')  98.7 us
    reduce_sum x1, other arithmetic, body(): ratio_grad = -jnp.sum(delta * out, -1)  14.1 us
    unnamed x93, local copies, waits for them, and re-layouts  11.3 us
    dot_general x1, matrix products, body(): jnp.einsum('nthd,nhrd->nthr', grad_num, state, precision=HIGHEST)  9.54 us
    ppermute x2, starting transfers between devices, passed_along(): lax.ppermute(value, axis, [(source, source + steps) for source in range(f...  8.35 us
  transfers between devices with their start and end apart: 4, of which 2 were waited for; matrix products, arithmetic and copies ran while one was open for 6% of the time, Pallas kernels for 0%

profile of v1, /device:TPU:0, one launch (start us, length us, event | category | flops | bytes accessed | tf_op | source)
XLA Modules:
  0.0 401.4 jit_solution(10032189386831203963)
XLA Ops:
  7.2 2.3 copy.332
  9.5 1.4 copy-done.4
  11.7 5.7 %collective-permute-start.1 = (bf16[128,16,128]{2,0,1:T(8,128)(2,1)}, bf16[128,16,128]{2,0,1:T(8,128)(2,1)}, u32[]{:S(2)}, u32[]{:S(2)}) collective-permute-start(bf16[128,16,128]{2,0,1:T(8,128)(2,1)} %slice_bitcast_fusion), channel_id=1, source_target_pairs={{0,4},{4,8},{8,12},{12,16},{16,20},{20,24},{24,28},{1,5},{5,9},{9,... | collective-permute-start | bytes 1572872 | tf_op jit(solution)/shard_map/ppermute | solution.py:16
  17.4 1.9 slice_bitcast_fusion.1
  19.3 2.7 collective-permute-start
  25.8 3.5 copy.177
  29.3 1.9 copy.171
  31.3 2.4 convert.3
  33.7 1.5 fusion.73
  35.2 2.0 fusion.65
  37.9 0.9 fusion.171
  39.6 1.9 pad_maximum_fusion
  41.5 1.5 copy-done.1
  43.0 2.1 fusion.44
  45.1 35.4 %all-gather = f32[128,8,128]{2,1,0:T(8,128)} all-gather(f32[16,8,128]{2,1,0:T(8,128)S(1)} %slice_reduce_fusion), channel_id=2, replica_groups=mesh['seq'=8,'batch'=4] {'seq'}, dimensions={0}, use_global_device_ids=true | all-gather | bytes 589824 | tf_op jit(solution)/shard_map/all_gather | solution.py:21
  80.6 30.6 %all-gather.4 = f32[8,16,8]{1,2,0:T(8,128)S(1)} all-gather(f32[1,16,8]{1,2,0:T(8,128)S(1)} %bitcast.246), channel_id=3, replica_groups=mesh['seq'=8,'batch'=4] {'seq'}, dimensions={0}, use_global_device_ids=true | all-gather | bytes 4608 | tf_op jit(solution)/shard_map/all_gather | solution.py:21
  111.2 7.7 %while.34 = (s32[]{:T(128)}, f32[16,8,128]{2,1,0:T(8,128)S(1)}, f32[16,8]{0,1:T(8,128)S(1)}, s32[]{:T(128)}, f32[8,16,8,128]{3,2,1,0:T(8,128)}, /*index=5*/f32[8,16,8]{1,2,0:T(8,128)S(1)}, s32[]{:T(128)}, s32[]{:T(128)}) while((s32[]{:T(128)}, f32[16,8,128]{2,1,0:T(8,128)S(1)}, f32[16,8]{0,1:T(8,128)S(1)}, s32[]{:T(128)}, ...), condition=%wide.region_5.6_spmd.clone, body=%wide.region_4.5_spmd.clone.sunk | while | flops 49540 | bytes 198259 | solution.py:34
  114.8 0.9 add_select_fusion.9
  115.7 0.9 add_select_fusion.9
  118.9 3.9 fusion.42
  124.9 6.7 %convolution_bitcast_fusion = f32[4,128,16,128]{3,1,2,0:T(8,128)S(1)} fusion(f32[4,16,8,128]{3,0,2,1:T(4,128)S(1)} %fusion.66, f32[512,16,8]{0,2,1:T(8,128)S(1)} %copy-done.13), kind=kOutput, calls=%fused_computation.42 | convolution fusion | flops 101056512 | bytes 4718592 | tf_op jit(solution)/shard_map/nthr,nhrd->nthd/dot_general | solution.py:155
  131.6 4.5 %copy.193 = f32[4,128,16,128]{3,2,1,0:T(8,128)} copy(f32[4,128,16,128]{3,1,2,0:T(8,128)S(1)} %convolution_bitcast_fusion) | data formatting | bytes 8388608 | tf_op jit(solution)/shard_map/nthr,nhrd->nthd/transpose | solution.py:155
  136.5 0.9 convolution_add_fusion.3
  138.2 1.7 pad_maximum_fusion.2
  139.9 2.9 fusion
  143.5 4.1 %fusion.2 = f32[4,16,128]{2,1,0:T(8,128)S(1)} fusion(f32[4,16,256,128]{3,2,1,0:T(8,128)S(1)} %get-tuple-element.359, f32[4,16,128]{2,1,0:T(8,128)S(1)} %get-tuple-element.358, pred[4,16,256]{2,1,0:T(8,128)(4,1)S(1)} %copy-done.26, pred[128,256]{0,1:T(8,128)(4,1)S(1)} %copy-done.21, pred[256]{0:T(512)(128)(4,1)S(1)} %copy-done.42), kind=kLoop, calls=%fused_computation.9 | loop fusion | flops 10477568 | bytes 8503552 | tf_op jit(solution)/shard_map/reduce_sum | solution.py:146
  148.4 1.7 fusion.32
  150.7 1.6 copy-done.10
  152.3 6.3 %fusion.27 = f32[4,128,16,128]{3,1,2,0:T(8,128)S(1)} fusion(f32[4,16,256,128]{3,2,1,0:T(8,128)S(1)} %copy-done.10, f32[4,16,128]{2,1,0:T(8,128)S(1)} %get-tuple-element.358, pred[4,16,256]{2,1,0:T(8,128)(4,1)S(1)} %copy-done.26, pred[128,256]{0,1:T(8,128)(4,1)S(1)} %copy-done.21, pred[256]{0:T(512)(128)(4,1)S(1)} %copy-done.42, ...), kind=kOutput, calls=%fused_computation.41 | convolution fusion | flops 555745280 | bytes 16859392 | tf_op jit(solution)/shard_map/nhqk,nkhd->nqhd/dot_general | solution.py:147
  158.6 4.4 %copy.180 = f32[4,128,16,128]{3,2,1,0:T(8,128)} copy(f32[4,128,16,128]{3,1,2,0:T(8,128)S(1)} %fusion.27) | data formatting | bytes 8388608 | tf_op jit(solution)/shard_map/nhqk,nkhd->nqhd/transpose | solution.py:147
  163.1 6.9 %fusion.14 = f32[512,16,128]{2,1,0:T(8,128)S(1)} fusion(f32[4,128,16,128]{3,2,1,0:T(8,128)} %copy.193, f32[4,128,16,128]{3,2,1,0:T(8,128)} %copy.180, f32[512,16]{1,0:T(8,128)S(1)} %copy.182, f32[512,16]{1,0:T(8,128)S(1)} %copy.198), kind=kLoop, calls=%fused_computation.21 | loop fusion | flops 3145728 | bytes 12648448 | tf_op jit(solution)/shard_map/div | solution.py:162
  170.0 14.1 %fusion.23 = f32[512,16]{1,0:T(8,128)S(1)} fusion(f32[512,16,128]{2,1,0:T(8,128)S(1)} %fusion.14, f32[512,16]{1,0:T(8,128)S(1)} %copy.198, bf16[1,512,16,128]{3,2,1,0:T(8,128)(2,1)S(1)} %copy-done.8), kind=kLoop, calls=%fused_computation.33 | loop fusion | flops 4186112 | bytes 6356992 | tf_op jit(solution)/shard_map/reduce_sum | solution.py:164
  185.1 0.9 fusion.122
  186.7 7.5 %fusion.174 = (f32[16,8,128]{2,1,0:T(8,128)S(1)}, f32[4,16,8,128]{3,2,1,0:T(8,128)}) fusion(f32[4,128,16,128]{3,2,1,0:T(8,128)} %convert.3, f32[4,128,16]{1,2,0:T(8,128)S(1)} %get-tuple-element.353, f32[4,128,16]{1,2,0:T(8,128)S(1)} %copy-done.28, f32[512,16,8]{0,2,1:T(8,128)S(1)} %copy-done.14), kind=kOutput, calls=%fused_computation.200 | convolution fusion | flops 103202816 | bytes 4849664 | tf_op jit(solution)/shard_map/nthr,nthd->nhrd/dot_general | solution.py:171
  194.2 31.2 %all-gather.2 = f32[128,8,128]{2,1,0:T(8,128)S(1)} all-gather(f32[16,8,128]{2,1,0:T(8,128)S(1)} %get-tuple-element.360), channel_id=4, replica_groups=mesh['seq'=8,'batch'=4] {'seq'}, dimensions={0}, use_global_device_ids=true | all-gather | bytes 589824 | tf_op jit(solution)/shard_map/all_gather | solution.py:21
  225.4 30.6 %all-gather.5 = f32[8,16,8]{1,2,0:T(8,128)S(1)} all-gather(f32[1,16,8]{1,2,0:T(8,128)S(1)} %bitcast.245), channel_id=5, replica_groups=mesh['seq'=8,'batch'=4] {'seq'}, dimensions={0}, use_global_device_ids=true | all-gather | bytes 4608 | tf_op jit(solution)/shard_map/all_gather | solution.py:21
  257.2 1.6 fusion.106
  258.7 2.6 convolution_add_fusion
  262.2 9.5 %fusion.76 = f32[4,128,16,8]{1,3,2,0:T(8,128)S(1)} fusion(f32[4,128,16,128]{3,2,1,0:T(8,128)} %convert.3, f32[4,128,16]{1,2,0:T(8,128)} %copy-done.31, f32[4,128,16]{1,2,0:T(8,128)} %get-tuple-element.354, f32[4,16,8,128]{3,0,2,1:T(4,128)} %copy-done.15, f32[4,16,8]{2,1,0:T(8,128)} %copy.207, f32[4,128,16]{1,2,0:T(8,128)} %copy-done.30), kind=kOutput, calls=%fused_computation.74 | convolution fusion | flops 102891520 | bytes 4818944 | tf_op jit(solution)/shard_map/nthd,nhrd->nthr/dot_general | solution.py:168
  271.7 2.0 fusion.79
  273.7 4.1 %fusion.51 = f32[5,128,16,8]{1,3,2,0:T(8,128)S(1)} fusion(bf16[5,128,16,128]{3,2,1,0:T(8,128)(2,1)S(1)} %bitcast.225, f32[5,16,8,128]{3,0,2,1:T(8,128)S(1)} %copy-done.16, f32[5,16,8]{2,1,0:T(8,128)S(1)} %copy.214), kind=kOutput, calls=%fused_computation.62 | convolution fusion | flops 125911040 | bytes 3279360 | tf_op jit(solution)/shard_map/nhrd,nthd->nthr/dot_general | solution.py:193
  277.9 4.1 %fusion.57 = f32[5,128,16,8]{1,3,2,0:T(8,128)S(1)} fusion(bf16[5,128,16,128]{3,2,1,0:T(8,128)(2,1)S(1)} %bitcast.226, f32[5,16,8,128]{3,0,2,1:T(8,128)S(1)} %fusion.106, f32[5,16,8]{2,1,0:T(8,128)S(1)} %copy.219), kind=kOutput, calls=%fused_computation.64 | convolution fusion | flops 125911040 | bytes 3279360 | tf_op jit(solution)/shard_map/nhrd,nthd->nthr/dot_general | solution.py:194
  282.1 3.1 fusion.47
  285.2 31.8 %all-reduce.8.cloned.1.call-done = (f32[16,128,8]{1,2,0:T(8,128)}, f32[16,128,8]{1,2,0:T(8,128)}) async-done(((f32[16,128,8]{1,2,0:T(8,128)}, f32[16,128,8]{1,2,0:T(8,128)}), (f32[16,128,8]{1,2,0:T(8,128)}, f32[16,128,8]{1,2,0:T(8,128)})) %all-reduce.8.cloned.1.call-update) | async-done | bytes 131088 | tf_op jit(solution)/shard_map/psum | solution.py:202
  317.0 7.2 %fusion.18 = bf16[1,512,16,128]{3,2,1,0:T(8,128)(2,1)} fusion(f32[512,16]{1,0:T(8,128)S(1)} %copy.198, f32[512,16]{1,0:T(8,128)S(1)} %copy.182, f32[1,512,16,128]{3,2,1,0:T(8,128)} %bitcast.221, f32[1,512,16,128]{3,2,1,0:T(8,128)} %bitcast.222), kind=kLoop, calls=%fused_computation.27 | loop fusion | flops 4194304 | bytes 10551296 | tf_op jit(solution)/shard_map/convert_element_type | solution.py:203
  324.3 66.9 %all-reduce.6.cloned.1.call-done = (f32[16,128,8]{1,2,0:T(8,128)}, f32[16,128,8]{1,2,0:T(8,128)}) async-done(((f32[16,128,8]{1,2,0:T(8,128)}, f32[16,128,8]{1,2,0:T(8,128)}), (f32[16,128,8]{1,2,0:T(8,128)}, f32[16,128,8]{1,2,0:T(8,128)})) %all-reduce.6.cloned.1.call-update) | async-done | bytes 131088 | tf_op jit(solution)/shard_map/psum | solution.py:202
  391.2 1.5 copy.355
  392.7 1.5 copy.356
  (173 shorter events, 20.7 us)
Async XLA Ops:
  7.2 26.5 %copy-start = (bf16[1,512,16,128]{3,2,1,0:T(8,128)(2,1)S(1)}, bf16[1,512,16,128]{3,2,1,0:T(8,128)(2,1)}, u32[]{:S(2)}) copy-start(bf16[1,512,16,128]{3,2,1,0:T(8,128)(2,1)} %param.11) | copy-start | bytes 6291460
  7.2 16.6 %copy-start.37 = (s32[1,16,32]{2,1,0:T(8,128)S(1)}, s32[1,16,32]{2,1,0:T(8,128)}, u32[]{:S(2)}) copy-start(s32[1,16,32]{2,1,0:T(8,128)} %param.14) | copy-start | bytes 6148
  7.2 309.8 %all-reduce.8.cloned.1.call-start = ((), (), s32[]{:S(2)}) async-start(), calls=%async_computation.1 | async-start | bytes 262144 | tf_op jit(solution)/shard_map/psum | solution.py:202
  9.5 1.4 copy-start.4
  11.7 23.5 %collective-permute-start.1 = (bf16[128,16,128]{2,0,1:T(8,128)(2,1)}, bf16[128,16,128]{2,0,1:T(8,128)(2,1)}, u32[]{:S(2)}, u32[]{:S(2)}) collective-permute-start(bf16[128,16,128]{2,0,1:T(8,128)(2,1)} %slice_bitcast_fusion), channel_id=1, source_target_pairs={{0,4},{4,8},{8,12},{12,16},{16,20},{20,24},{24,28},{1,5},{5,9},{9,... | collective-permute-start | bytes 1572872 | tf_op jit(solution)/shard_map/ppermute | solution.py:16
  19.3 20.3 %collective-permute-start = (bf16[128,16,128]{2,1,0:T(8,128)(2,1)}, bf16[128,16,128]{2,1,0:T(8,128)(2,1)S(1)}, u32[]{:S(2)}, u32[]{:S(2)}) collective-permute-start(bf16[128,16,128]{2,1,0:T(8,128)(2,1)} %slice_bitcast_fusion.1), channel_id=1, source_target_pairs={{0,4},{4,8},{8,12},{12,16},{16,20},{20,24},{24,28},{1,5},{5,9},{9,... | collective-permute-start | bytes 1572872 | tf_op jit(solution)/shard_map/ppermute | solution.py:16
  22.0 15.2 %copy-start.32 = (f32[640]{0:T(1024)}, f32[640]{0:T(1024)S(1)}, u32[]{:S(2)}) copy-start(f32[640]{0:T(1024)S(1)} %fusion.149) | copy-start | bytes 7684
  22.0 114.2 %copy-start.34 = (s32[4]{0:T(128)}, s32[4]{0:T(128)S(1)}, u32[]{:S(2)}) copy-start(s32[4]{0:T(128)S(1)} %iota_add_fusion.1) | copy-start | bytes 52
  25.2 4.1 %copy-start.3 = (bf16[1,512,16,128]{3,2,1,0:T(8,128)(2,1)S(1)}, bf16[1,512,16,128]{3,2,1,0:T(8,128)(2,1)}, u32[]{:S(2)}) copy-start(bf16[1,512,16,128]{3,2,1,0:T(8,128)(2,1)} %param.13) | copy-start | bytes 6291460
  29.3 1.9 copy-start.7
  31.2 2.4 copy-start.27
  31.2 3.9 copy-start.5
  31.2 3.9 copy-start.44
  33.6 3.5 copy-start.19
  39.6 3.4 copy-start.12
  41.5 1.5 copy-start.1
  111.2 12.2 %copy-start.38 = (f32[5]{0:T(128)S(1)}, f32[5]{0:T(128)}, u32[]{:S(2)}) copy-start(f32[5]{0:T(128)} %broadcast_subtract_fusion) | copy-start | bytes 64
  111.2 12.2 %copy-start.40 = (f32[5]{0:T(128)S(1)}, f32[5]{0:T(128)}, u32[]{:S(2)}) copy-start(f32[5]{0:T(128)} %compare_convert_fusion.1) | copy-start | bytes 64
  118.8 6.0 %copy-start.13 = (f32[512,16,8]{0,2,1:T(8,128)S(1)}, f32[512,16,8]{0,2,1:T(8,128)}, u32[]{:S(2)}) copy-start(f32[512,16,8]{0,2,1:T(8,128)} %fusion.73) | copy-start | bytes 786436
  124.1 0.8 copy-start.15
  131.6 4.7 %copy-start.29 = (f32[5,16,8]{1,0,2:T(8,128)S(1)}, f32[5,16,8]{1,0,2:T(8,128)}, u32[]{:S(2)}) copy-start(f32[5,16,8]{1,0,2:T(8,128)} %copy.195) | copy-start | bytes 7684
  131.6 5.9 %copy-start.14 = (f32[512,16,8]{0,2,1:T(8,128)S(1)}, f32[512,16,8]{0,2,1:T(8,128)}, u32[]{:S(2)}) copy-start(f32[512,16,8]{0,2,1:T(8,128)} %fusion.73) | copy-start | bytes 786436
  137.5 2.4 copy-start.11
  137.5 2.4 copy-start.21
  137.5 2.4 copy-start.26
  137.5 2.4 copy-start.42
  138.2 10.1 %copy-start.23 = (f32[4,16,1,128]{3,2,1,0:T(1,128)}, f32[4,16,1,128]{3,2,1,0:T(1,128)S(1)}, u32[]{:S(2)}) copy-start(f32[4,16,1,128]{3,2,1,0:T(1,128)S(1)} %fusion.112) | copy-start | bytes 98308
  142.8 4.8 %copy-start.9 = (f32[4,16,256,128]{3,2,1,0:T(8,128)}, f32[4,16,256,128]{3,2,1,0:T(8,128)S(1)}, u32[]{:S(2)}) copy-start(f32[4,16,256,128]{3,2,1,0:T(8,128)S(1)} %get-tuple-element.359) | copy-start | bytes 25165828
  148.4 3.9 copy-start.10
  158.6 4.4 %copy-start.22 = (f32[4,2,8,128]{3,2,0,1:T(8,128)S(1)}, f32[4,2,8,128]{3,2,0,1:T(8,128)}, u32[]{:S(2)}) copy-start(f32[4,2,8,128]{3,2,0,1:T(8,128)} %copy.331) | copy-start | bytes 98308
  163.1 6.9 %copy-start.8 = (bf16[1,512,16,128]{3,2,1,0:T(8,128)(2,1)S(1)}, bf16[1,512,16,128]{3,2,1,0:T(8,128)(2,1)}, u32[]{:S(2)}) copy-start(bf16[1,512,16,128]{3,2,1,0:T(8,128)(2,1)} %param.17) | copy-start | bytes 6291460
  170.0 14.2 %copy-start.24 = (f32[4,16,1,128]{3,2,1,0:T(1,128)S(1)}, f32[4,16,1,128]{3,2,1,0:T(1,128)}, u32[]{:S(2)}) copy-start(f32[4,16,1,128]{3,2,1,0:T(1,128)} %copy-done.23) | copy-start | bytes 98308
  170.0 15.0 %copy-start.35 = (s32[4]{0:T(128)S(1)}, s32[4]{0:T(128)}, u32[]{:S(2)}) copy-start(s32[4]{0:T(128)} %copy-done.34) | copy-start | bytes 52
  170.0 16.6 %copy-start.28 = (f32[4,128,16]{1,2,0:T(8,128)S(1)}, f32[4,128,16]{1,2,0:T(8,128)}, u32[]{:S(2)}) copy-start(f32[4,128,16]{1,2,0:T(8,128)} %get-tuple-element.354) | copy-start | bytes 98308
  184.2 9.9 %copy-start.30 = (f32[4,128,16]{1,2,0:T(8,128)}, f32[4,128,16]{1,2,0:T(8,128)S(1)}, u32[]{:S(2)}) copy-start(f32[4,128,16]{1,2,0:T(8,128)S(1)} %get-tuple-element.352) | copy-start | bytes 98308
  184.3 9.9 %copy-start.31 = (f32[4,128,16]{1,2,0:T(8,128)}, f32[4,128,16]{1,2,0:T(8,128)S(1)}, u32[]{:S(2)}) copy-start(f32[4,128,16]{1,2,0:T(8,128)S(1)} %get-tuple-element.353) | copy-start | bytes 98308
  186.6 69.3 %copy-start.25 = (f32[16,8]{0,1:T(8,128)S(1)}, f32[16,8]{0,1:T(8,128)}, u32[]{:S(2)}) copy-start(f32[16,8]{0,1:T(8,128)} %custom-call.3) | copy-start | bytes 1540
  186.6 70.1 %copy-start.36 = (s32[4]{0:T(128)S(1)}, s32[4]{0:T(128)}, u32[]{:S(2)}) copy-start(s32[4]{0:T(128)} %copy-done.34) | copy-start | bytes 52
  186.6 70.1 %copy-start.39 = (f32[5]{0:T(128)S(1)}, f32[5]{0:T(128)}, u32[]{:S(2)}) copy-start(f32[5]{0:T(128)} %broadcast_subtract_fusion) | copy-start | bytes 64
  186.6 70.1 %copy-start.41 = (f32[5]{0:T(128)S(1)}, f32[5]{0:T(128)}, u32[]{:S(2)}) copy-start(f32[5]{0:T(128)} %compare_convert_fusion.1) | copy-start | bytes 64
  186.6 70.1 %copy-start.43 = (f32[5]{0:T(128)S(1)}, f32[5]{0:T(128)}, u32[]{:S(2)}) copy-start(f32[5]{0:T(128)} %compare_convert_fusion) | copy-start | bytes 64
  271.7 2.0 copy-start.2
  271.7 2.0 copy-start.16
  277.9 4.2 %copy-start.6 = (bf16[1,512,16,128]{3,1,2,0:T(8,128)(2,1)S(1)}, bf16[1,512,16,128]{3,1,2,0:T(8,128)(2,1)}, u32[]{:S(2)}) copy-start(bf16[1,512,16,128]{3,1,2,0:T(8,128)(2,1)} %copy-done.4) | copy-start | bytes 6291460
  277.9 4.2 %copy-start.18 = (f32[640,16,8]{0,2,1:T(8,128)S(1)}, f32[640,16,8]{0,2,1:T(8,128)}, u32[]{:S(2)}) copy-start(f32[640,16,8]{0,2,1:T(8,128)} %copy-done.17) | copy-start | bytes 983044
  277.9 4.2 %copy-start.20 = (f32[640,16]{0,1:T(8,128)S(1)}, f32[640,16]{0,1:T(8,128)}, u32[]{:S(2)}) copy-start(f32[640,16]{0,1:T(8,128)} %copy-done.19) | copy-start | bytes 122884
  277.9 4.2 %copy-start.33 = (f32[640]{0:T(1024)S(1)}, f32[640]{0:T(1024)}, u32[]{:S(2)}) copy-start(f32[640]{0:T(1024)} %copy-done.32) | copy-start | bytes 7684
  285.2 106.0 %all-reduce.6.cloned.1.call-start = ((), (), s32[]{:S(2)}) async-start(), calls=%async_computation | async-start | bytes 262144 | tf_op jit(solution)/shard_map/psum | solution.py:202
  (1 other events, 0.8 us)
Sparse Core Ops, SparseCore 0:
  285.3 31.6 all-reduce.7
  320.5 70.6 all-reduce.5
